TPU v7x, 32 devices: a whole 2x2x4 slice. The times are simulated.
32 devices in a mesh: row: 4 (over y, x), col: 8 (over z, core).
Axes of the slice: x: 2, y: 2, z: 4, core: 2. Of those that a mesh axis runs over, the one named last changes fastest.
Arguments:
- pair: float32 [512, 512, 128], P('row', 'col'), may hold values from -6 to 6
- in_gain: float32 [2, 128], replicated, may hold values from 1 to 4
- in_bias: float32 [2, 128], replicated, may hold values from -1.5 to 1.5
- proj_weight: bfloat16 [2, 128, 640], replicated, may hold values from -0.5 to 0.5
- proj_bias: float32 [2, 640], replicated, may hold values from -1.5 to 1.5
- mid_gain: float32 [2, 128], replicated, may hold values from 0.5 to 2
- mid_bias: float32 [2, 128], replicated, may hold values from -3 to 3
- out_weight: bfloat16 [2, 128, 128], replicated, may hold values from -0.5 to 0.5
- out_bias: float32 [2, 128], replicated, may hold values from -3 to 3
Outputs:
- updated: float32 [512, 512, 128], P('row', 'col')
All inputs are finite; a program needn't handle non-finite values.
Results may differ from a plain program's by a relative error of at most 0.015.
Values may be sent and summed in bfloat16 or wider, within the bound.
A program may use at most 128 MiB of HBM per device.

v0:
```python
import jax
import jax.numpy as jnp
from jax import lax
from jax.sharding import PartitionSpec as P


def layer_norm(values, gain, offset):
    mean = jnp.mean(values, -1, keepdims=True)
    centred = values - mean
    variance = jnp.mean(centred * centred, -1, keepdims=True)
    return centred * lax.rsqrt(variance + 1e-05) * gain + offset


def projections(state, update, in_gain, in_bias, proj_weight, proj_bias):
    hidden = (proj_weight.shape[2] - state.shape[2]) // 4
    normed = layer_norm(state, in_gain[update], in_bias[update]).astype(jnp.bfloat16)
    proj = (
        jnp.dot(normed, proj_weight[update], preferred_element_type=jnp.float32) + proj_bias[update]
    )
    left = (jax.nn.sigmoid(proj[..., hidden : 2 * hidden]) * proj[..., 0:hidden]).astype(
        jnp.bfloat16
    )
    right = (
        jax.nn.sigmoid(proj[..., 3 * hidden : 4 * hidden]) * proj[..., 2 * hidden : 3 * hidden]
    ).astype(jnp.bfloat16)
    gate = jax.nn.sigmoid(proj[..., 4 * hidden :])
    left_major = jnp.transpose(left, (2, 0, 1))
    right_major = jnp.transpose(right, (2, 0, 1))
    return (left_major, right_major, gate)


def finish(state, mixed_major, gate, update, mid_gain, mid_bias, out_weight, out_bias):
    mixed = jnp.transpose(mixed_major, (1, 2, 0))
    middle = layer_norm(mixed, mid_gain[update], mid_bias[update]).astype(jnp.bfloat16)
    outcome = (
        jnp.dot(middle, out_weight[update], preferred_element_type=jnp.float32) + out_bias[update]
    )
    return state + gate * outcome


def body(pair, in_gain, in_bias, proj_weight, proj_bias, mid_gain, mid_bias, out_weight, out_bias):
    left, right, gate = projections(pair, 0, in_gain, in_bias, proj_weight, proj_bias)
    terms = jnp.einsum(
        "cjk,cik->cji",
        lax.all_gather(right, "row", axis=1, tiled=True),
        left,
        preferred_element_type=jnp.float32,
    )
    summed = lax.psum_scatter(
        terms.astype(jnp.bfloat16), "col", scatter_dimension=1, tiled=True
    ).astype(jnp.float32)
    mixed = jnp.transpose(summed, (0, 2, 1))
    state = finish(pair, mixed, gate, 0, mid_gain, mid_bias, out_weight, out_bias)
    left, right, gate = projections(state, 1, in_gain, in_bias, proj_weight, proj_bias)
    terms = jnp.einsum(
        "cki,ckj->cij",
        lax.all_gather(left, "col", axis=2, tiled=True),
        right,
        preferred_element_type=jnp.float32,
    )
    mixed = lax.psum_scatter(
        terms.astype(jnp.bfloat16), "row", scatter_dimension=1, tiled=True
    ).astype(jnp.float32)
    return finish(state, mixed, gate, 1, mid_gain, mid_bias, out_weight, out_bias)


def solution(mesh):
    placed = (P("row", "col", None), P(), P(), P(), P(), P(), P(), P(), P())
    return jax.shard_map(
        body, mesh=mesh, in_specs=placed, out_specs=P("row", "col", None), check_vma=False
    )
```

profile of v0, /device:TPU:25, one launch (start us, length us, event | category | flops | bytes accessed | tf_op | source)
XLA Modules:
  0.0 713.8 jit_solution(10569726767375424847)
XLA Ops:
  6.5 0.0 all-gather.3.cloned.1.call-start
  6.5 0.8 slice_reduce_fusion
  7.3 0.0 copy-start.7
  7.3 0.0 copy-start.8
  7.3 3.3 reduce_sum.72
  10.7 0.1 copy.65
  10.8 0.1 copy.66
  10.9 4.0 multiply_reduce_fusion.1
  14.8 0.0 copy-start.5
  14.9 0.1 copy.67
  15.0 0.1 copy.68
  15.1 0.0 copy-done.7
  15.1 0.0 copy-done.8
  15.1 5.8 add_convert_fusion.1
  20.9 0.0 copy-done.5
  20.9 4.0 broadcast_add_fusion.1
  24.9 0.0 copy-start.1
  24.9 4.3 fusion.51
  29.2 3.9 copy-done.1
  33.1 0.0 all-gather.3.cloned.1.call-update
  33.2 0.0 reduce-scatter.5.cloned.1.call-start
  33.2 3.3 copy.71
  36.5 85.1 %all-gather.3.cloned.1.call-done = bf16[128,512,64]{0,1,2:T(8,128)(2,1)} async-done(((bf16[128,128,64]{0,1,2:T(8,128)(2,1)}), bf16[128,512,64]{0,1,2:T(8,128)(2,1)}) %all-gather.3.cloned.1.call-update) | async-done | bytes 8388624 | tf_op jit(solution)/shard_map/all_gather | solution.py:45
  121.6 12.5 %copy.70 = bf16[128,512,64]{1,2,0:T(8,128)(2,1)} copy(bf16[128,512,64]{0,1,2:T(8,128)(2,1)} %all-gather.3.cloned.1.call-done) | data formatting | bytes 16777216 | tf_op jit(solution)/shard_map/all_gather | solution.py:45
  134.1 10.4 %convolution_convert_fusion = bf16[128,512,128]{2,1,0:T(8,128)(2,1)} fusion(bf16[128,512,64]{1,2,0:T(8,128)(2,1)} %copy.70, bf16[128,128,64]{1,2,0:T(8,128)(2,1)S(1)} %copy.71), kind=kOutput, calls=%fused_computation.4 | convolution fusion | flops 1082130432 | bytes 27262976 | tf_op jit(solution)/shard_map/cjk,cik->cji/dot_general | solution.py:43
  144.5 0.0 copy-start.6
  144.5 0.0 reduce-scatter.5.cloned.1.call-update
  144.5 0.3 all-gather.5.cloned.1.call-start
  144.8 0.3 copy-done.6
  145.2 0.0 copy-done.9
  145.2 0.0 copy-done.10
  145.2 165.1 %reduce-scatter.5.cloned.1.call-done = bf16[128,64,128]{2,1,0:T(8,128)(2,1)} async-done(((bf16[128,512,128]{2,1,0:T(8,128)(2,1)}), bf16[128,64,128]{2,1,0:T(8,128)(2,1)}) %reduce-scatter.5.cloned.1.call-update) | async-done | bytes 2097168 | tf_op jit(solution)/shard_map/reduce_scatter | solution.py:49
  310.3 2.1 bitcast_reduce_fusion.1
  312.4 2.2 fusion.39
  314.6 2.5 fusion.42
  317.1 0.0 copy-done.11
  317.1 0.0 copy-done.2
  317.1 10.9 %fusion.62 = (f32[128,64]{0,1:T(8,128)S(1)}, f32[128,64,128]{2,0,1:T(8,128)S(1)}) fusion(f32[128]{0:T(128)S(1)} %get-tuple-element.12, bf16[2,128,128]{2,1,0:T(8,128)(2,1)S(1)} %copy-done.11, bf16[128,64,128]{0,1,2:T(8,128)(2,1)S(1)} %fusion.42, f32[128,64,640]{2,0,1:T(8,128)} %copy-done.1, f32[128,64,128]{2,1,0:T(8,128)S(1)} %copy-done.2), kind=kOutput, calls=%fused_computation.101 | convolution fusion | flops 275767296 | bytes 14746112 | tf_op jit(solution)/shard_map/dot_general | solution.py:36
  328.0 0.0 copy-start.3
  328.0 2.6 multiply_reduce_fusion
  330.7 3.5 broadcast_add_fusion
  334.2 0.0 copy-done.3
  334.2 0.0 copy-start
  334.2 4.4 fusion.52
  338.6 3.9 copy-done
  342.4 4.1 copy.76
  346.5 0.0 all-gather.5.cloned.1.call-update
  346.5 0.0 reduce-scatter.7.cloned.1.call-start
  346.6 3.3 copy.78
  349.9 146.4 %all-gather.5.cloned.1.call-done = bf16[128,128,512]{1,0,2:T(8,128)(2,1)} async-done(((bf16[128,128,64]{1,0,2:T(8,128)(2,1)}), bf16[128,128,512]{1,0,2:T(8,128)(2,1)}) %all-gather.5.cloned.1.call-update) | async-done | bytes 16777232 | tf_op jit(solution)/shard_map/all_gather | solution.py:57
  496.3 52.6 %fusion.2 = bf16[128,512,64]{1,2,0:T(8,128)(2,1)} fusion(bf16[128,128,64]{1,2,0:T(8,128)(2,1)S(1)} %copy.78, bf16[128,128,512]{1,0,2:T(8,128)(2,1)} %all-gather.5.cloned.1.call-done), kind=kOutput, calls=%fused_computation.5 | convolution fusion | flops 1077936128 | bytes 27262976 | tf_op jit(solution)/shard_map/cki,ckj->cij/dot_general | solution.py:55
  548.9 24.0 %copy.82 = bf16[128,512,64]{2,0,1:T(8,128)(2,1)} copy(bf16[128,512,64]{1,2,0:T(8,128)(2,1)} %fusion.2) | data formatting | bytes 16777216
  572.9 22.5 %reshape.64 = bf16[512,8192]{1,0:T(8,128)(2,1)} reshape(bf16[512,128,64]{2,1,0:T(8,128)(2,1)} %bitcast.83) | data formatting | bytes 16777216
  595.4 0.0 reduce-scatter.7.cloned.1.call-update
  595.4 87.1 %reduce-scatter.7.cloned.1.call-done = bf16[128,8192]{1,0:T(8,128)(2,1)} async-done(((bf16[512,8192]{1,0:T(8,128)(2,1)}), bf16[128,8192]{1,0:T(8,128)(2,1)}) %reduce-scatter.7.cloned.1.call-update) | async-done | bytes 2097168
  682.6 6.9 reshape.65
  689.5 5.6 copy.83
  695.1 0.0 copy-start.4
  695.1 0.4 bitcast_reduce_fusion
  695.5 0.6 fusion.33
  696.1 0.9 fusion.36
  697.0 0.3 copy-done.4
  697.3 5.2 fusion.17
  702.5 4.4 copy.80
  (15 shorter events, 0.1 us)
Async XLA Ops:
  6.5 115.1 %all-gather.3.cloned.1.call-start = ((), (), s32[]{:S(2)}) async-start(), calls=%async_computation.2 | async-start | bytes 10485760 | tf_op jit(solution)/shard_map/all_gather | solution.py:45
  7.3 7.7 %copy-start.7 = (f32[2,128]{1,0:T(2,128)S(1)}, f32[2,128]{1,0:T(2,128)}, u32[]{:S(2)}) copy-start(f32[2,128]{1,0:T(2,128)} %param.11) | copy-start | bytes 3076
  7.3 7.7 %copy-start.8 = (f32[2,128]{1,0:T(2,128)S(1)}, f32[2,128]{1,0:T(2,128)}, u32[]{:S(2)}) copy-start(f32[2,128]{1,0:T(2,128)} %param.10) | copy-start | bytes 3076
  14.8 6.0 copy-start.5
  24.9 8.2 %copy-start.1 = (f32[128,64,640]{2,0,1:T(8,128)}, f32[128,64,640]{2,0,1:T(8,128)S(1)}, u32[]{:S(2)}) copy-start(f32[128,64,640]{2,0,1:T(8,128)S(1)} %broadcast_add_fusion.1) | copy-start | bytes 62914564
  33.2 277.1 %reduce-scatter.5.cloned.1.call-start = ((), (), s32[]{:S(2)}) async-start(), calls=%async_computation.3 | async-start | bytes 18874368 | tf_op jit(solution)/shard_map/reduce_scatter | solution.py:49
  144.5 0.7 copy-start.6
  144.5 0.7 copy-start.9
  144.5 0.7 copy-start.10
  144.5 351.8 %all-gather.5.cloned.1.call-start = ((), (), s32[]{:S(2)}) async-start(), calls=%async_computation.4 | async-start | bytes 18874368 | tf_op jit(solution)/shard_map/all_gather | solution.py:57
  145.2 171.9 %copy-start.11 = (bf16[2,128,128]{2,1,0:T(8,128)(2,1)S(1)}, bf16[2,128,128]{2,1,0:T(8,128)(2,1)}, u32[]{:S(2)}) copy-start(bf16[2,128,128]{2,1,0:T(8,128)(2,1)} %param.16) | copy-start | bytes 196612
  310.3 6.8 copy-start.2
  328.0 6.2 copy-start.3
  334.2 8.2 %copy-start = (f32[128,64,640]{2,0,1:T(8,128)}, f32[128,64,640]{2,0,1:T(8,128)S(1)}, u32[]{:S(2)}) copy-start(f32[128,64,640]{2,0,1:T(8,128)S(1)} %broadcast_add_fusion) | copy-start | bytes 62914564
  346.5 336.0 %reduce-scatter.7.cloned.1.call-start = ((), (), s32[]{:S(2)}) async-start(), calls=%async_computation.5 | async-start | bytes 10485760
  695.1 2.2 copy-start.4
Sparse Core Ops, SparseCore 0:
  33.3 88.2 all-gather.2
  144.6 165.6 reduce-scatter.4
  346.7 149.6 all-gather.4
  595.6 86.9 reduce-scatter.6
where the time goes:
time: 726 us; the launch traced here: 714 us
  waiting for transfers between devices  484 us (67%)
  local copies, waits for them, and re-layouts  96.3 us (13%)
  matrix products  86.6 us (12%)
  other arithmetic  33 us (5%)
  between operations  13.8 us (2%)
    reduce_scatter x1, waiting for transfers between devices, body(): lax.psum_scatter(terms.astype(jnp.bfloat16), 'col', scatter_dimension=1,...  165 us
    all_gather x1, waiting for transfers between devices, body(): lax.all_gather(left, 'col', axis=2, tiled=True)  146 us
    unnamed x5, waiting for transfers between devices  87.2 us
    all_gather x1, waiting for transfers between devices, body(): lax.all_gather(right, 'row', axis=1, tiled=True)  85.1 us
    unnamed x28, local copies, waits for them, and re-layouts  67.6 us
    dot_general x1, matrix products, body(): jnp.einsum('cki,ckj->cij', lax.all_gather(left, 'col', axis=2, tiled=True...  52.6 us
    dot_general x2, matrix products, finish(): jnp.dot(middle, out_weight[update], preferred_element_type=jnp.float32)  16.1 us
  transfers between devices with their start and end apart: 4, of which 4 were waited for; matrix products, arithmetic and copies ran while one was open for 1% of the time, Pallas kernels for 0%

commit v1 on v0

--- a/solution.py
+++ b/solution.py
@@ -1,7 +1,176 @@
+import functools
+
 import jax
 import jax.numpy as jnp
 from jax import lax
+from jax.experimental import pallas as pl
+from jax.experimental.pallas import tpu as pltpu
 from jax.sharding import PartitionSpec as P
+
+MESH = pl.DeviceIdType.MESH
+
+
+def triangle_kernel(
+    update, rows, cols, left_ref, right_ref, out_ref, left_all, right_all, mixed_all,
+    send_sem, recv_sem, back_send_sem, back_recv_sem, local_sem,
+):
+    devices = rows * cols
+    row, col = lax.axis_index("row"), lax.axis_index("col")
+    me = row * cols + col
+
+    def place(offset):
+        other = lax.rem(me + offset, devices)
+        return other, lax.div(other, cols), lax.rem(other, cols)
+
+    barrier = pltpu.get_barrier_semaphore()
+
+    def greet(offset, carry):
+        _, r, c = place(offset)
+        pl.semaphore_signal(barrier, inc=1, device_id=(r, c), device_id_type=MESH)
+        return carry
+
+    lax.fori_loop(1, devices, greet, 0)
+    pl.semaphore_wait(barrier, devices - 1)
+
+    pairs = ((left_ref, left_all), (right_ref, right_all))
+
+    def outgoing(which, offset):
+        source, target = pairs[which]
+        other, r, c = place(offset)
+        return pltpu.make_async_remote_copy(
+            src_ref=source.at[other],
+            dst_ref=target.at[row, col],
+            send_sem=send_sem.at[which, other],
+            recv_sem=recv_sem.at[which, me],
+            device_id=(r, c),
+            device_id_type=MESH,
+        )
+
+    def incoming(which, offset):
+        source, target = pairs[which]
+        other, r, c = place(offset)
+        return pltpu.make_async_remote_copy(
+            src_ref=source.at[other],
+            dst_ref=target.at[r, c],
+            send_sem=send_sem.at[which, other],
+            recv_sem=recv_sem.at[which, other],
+            device_id=(r, c),
+            device_id_type=MESH,
+        )
+
+    def send(offset, carry):
+        outgoing(0, offset).start()
+        outgoing(1, offset).start()
+        return carry
+
+    lax.fori_loop(1, devices, send, 0)
+    own = [
+        pltpu.make_async_copy(source.at[me], target.at[row, col], local_sem.at[which])
+        for which, (source, target) in enumerate(pairs)
+    ]
+    for copy in own:
+        copy.start()
+    for copy in own:
+        copy.wait()
+
+    def receive(offset, carry):
+        incoming(0, offset).wait_recv()
+        incoming(1, offset).wait_recv()
+        return carry
+
+    lax.fori_loop(1, devices, receive, 0)
+
+    channels, depth, width = left_all.shape[2:]
+
+    def whole(ref, channel):
+        return jnp.concatenate(
+            [ref[r, :, channel].reshape(cols * depth, width) for r in range(rows)], axis=1
+        )
+
+    def product(channel, carry):
+        contract = ((0,), (0,)) if update == 0 else ((1,), (1,))
+        mixed = lax.dot_general(
+            whole(right_all, channel),
+            whole(left_all, channel),
+            (contract, ((), ())),
+            preferred_element_type=jnp.float32,
+        ).astype(jnp.bfloat16)
+        for r in range(rows):
+            mixed_all[r, :, channel] = mixed[:, r * width : (r + 1) * width].reshape(
+                cols, depth, width
+            )
+        return carry
+
+    lax.fori_loop(0, channels, product, 0)
+
+    def outgoing_back(offset):
+        other, r, c = place(offset)
+        return pltpu.make_async_remote_copy(
+            src_ref=mixed_all.at[r, c],
+            dst_ref=out_ref.at[me],
+            send_sem=back_send_sem.at[other],
+            recv_sem=back_recv_sem.at[me],
+            device_id=(r, c),
+            device_id_type=MESH,
+        )
+
+    def incoming_back(offset):
+        other, r, c = place(offset)
+        return pltpu.make_async_remote_copy(
+            src_ref=mixed_all.at[r, c],
+            dst_ref=out_ref.at[other],
+            send_sem=back_send_sem.at[other],
+            recv_sem=back_recv_sem.at[other],
+            device_id=(r, c),
+            device_id_type=MESH,
+        )
+
+    def send_back(offset, carry):
+        outgoing_back(offset).start()
+        return carry
+
+    lax.fori_loop(1, devices, send_back, 0)
+    last = pltpu.make_async_copy(mixed_all.at[row, col], out_ref.at[me], local_sem.at[0])
+    last.start()
+    last.wait()
+
+    def finish_all(offset, carry):
+        incoming_back(offset).wait_recv()
+        outgoing_back(offset).wait_send()
+        outgoing(0, offset).wait_send()
+        outgoing(1, offset).wait_send()
+        return carry
+
+    lax.fori_loop(1, devices, finish_all, 0)
+
+
+def triangle(update, rows, cols, left, right):
+    devices = rows * cols
+    channels, depth, width = left.shape
+    split = (devices, channels // devices, depth, width)
+    held = (rows, cols) + split[1:]
+    anywhere = pl.BlockSpec(memory_space=pl.ANY)
+    mixed = pl.pallas_call(
+        functools.partial(triangle_kernel, update, rows, cols),
+        out_shape=jax.ShapeDtypeStruct(split, jnp.bfloat16),
+        in_specs=[anywhere] * 2,
+        out_specs=anywhere,
+        scratch_shapes=[
+            pltpu.VMEM(held, jnp.bfloat16),
+            pltpu.VMEM(held, jnp.bfloat16),
+            pltpu.VMEM(held, jnp.bfloat16),
+            pltpu.SemaphoreType.DMA((2, devices)),
+            pltpu.SemaphoreType.DMA((2, devices)),
+            pltpu.SemaphoreType.DMA((devices,)),
+            pltpu.SemaphoreType.DMA((devices,)),
+            pltpu.SemaphoreType.DMA((2,)),
+        ],
+        compiler_params=pltpu.CompilerParams(
+            collective_id=update, has_side_effects=True, vmem_limit_bytes=32 * 1024 * 1024
+        ),
+        name=f"triangle_{update}",
+    )(left.reshape(split), right.reshape(split))
+    return mixed.reshape(left.shape)
 
 
 def layer_norm(values, gain, offset):
@@ -64,8 +233,32 @@
     return finish(state, mixed, gate, 1, mid_gain, mid_bias, out_weight, out_bias)
 
 
+def channel_body(
+    rows, cols, pair, in_gain, in_bias, proj_weight, proj_bias, mid_gain, mid_bias, out_weight,
+    out_bias,
+):
+    state = pair
+    for update in range(2):
+        left, right, gate = projections(state, update, in_gain, in_bias, proj_weight, proj_bias)
+        mixed = triangle(
+            update, rows, cols, jnp.transpose(left, (0, 2, 1)), jnp.transpose(right, (0, 2, 1))
+        )
+        mixed = jnp.transpose(mixed.astype(jnp.float32), (0, 2, 1))
+        state = finish(state, mixed, gate, update, mid_gain, mid_bias, out_weight, out_bias)
+    return state
+
+
 def solution(mesh):
     placed = (P("row", "col", None), P(), P(), P(), P(), P(), P(), P(), P())
-    return jax.shard_map(
-        body, mesh=mesh, in_specs=placed, out_specs=P("row", "col", None), check_vma=False
-    )
+    rows, cols = mesh.shape["row"], mesh.shape["col"]
+
+    def run(*arrays):
+        hidden = arrays[7].shape[1]
+        local = functools.partial(channel_body, rows, cols)
+        if hidden % (rows * cols) != 0:
+            local = body
+        return jax.shard_map(
+            local, mesh=mesh, in_specs=placed, out_specs=P("row", "col", None), check_vma=False
+        )(*arrays)
+
+    return run

time: 726 us -> 403 us (0.56); the launches traced: 714 us -> 402 us
  waiting for transfers between devices: 484 us -> 0 us
  Pallas kernels: 0 us -> 291 us
  matrix products: 86.6 us -> 23.1 us
  local copies, waits for them, and re-layouts: 96.3 us -> 44.5 us
  between operations: 13.8 us -> 0.3 us
  other arithmetic: 33 us -> 43.4 us
    pallas_call x0 -> x2, Pallas kernels: none -> 291 us  [triangle(): pl.pallas_call(functools.partial(triangle_kernel, update, rows, cols), ou...]
    all_gather x2 -> x0, waiting for transfers between devices: 232 us -> none  [the longest x1 146 us: body(): lax.all_gather(left, 'col', axis=2, tiled=True)]
    reduce_scatter x1 -> x0, waiting for transfers between devices: 165 us -> none  [body(): lax.psum_scatter(terms.astype(jnp.bfloat16), 'col', scatter_dimension=1,...]
    unnamed x5 -> x0, waiting for transfers between devices: 87.2 us -> none
    dot_general x2 -> x0, matrix products: 63 us -> none  [the longest x1 52.6 us: body(): jnp.einsum('cki,ckj->cij', lax.all_gather(left, 'col', axis=2, tiled=True...]
    unnamed x28 -> x22, local copies, waits for them, and re-layouts: 67.6 us -> 11 us
    another operation x0 -> x6, local copies, waits for them, and re-layouts: none -> 25.7 us  [the longest x2 10.8 us: finish(): mixed = jnp.transpose(mixed_major, (1, 2, 0))]
    another operation x0 -> x4, other arithmetic: none -> 13.8 us  [the longest x2 8.65 us: channel_body(): jnp.transpose(right, (0, 2, 1))]
  transfers between devices with their start and end apart: 4 -> 0, of which waited for: 4 -> 0; matrix products, arithmetic and copies ran while one was open for 1% -> 0% of each run, Pallas kernels for 0% -> 0%
where the time goes in v1:
time: 403 us; the launch traced here: 402 us
  Pallas kernels  291 us (72%)
  local copies, waits for them, and re-layouts  44.5 us (11%)
  other arithmetic  43.4 us (11%)
  matrix products  23.1 us (6%)
    pallas_call x2, Pallas kernels, triangle(): pl.pallas_call(functools.partial(triangle_kernel, update, rows, cols), ou...  291 us
    dot_general x2, matrix products, finish(): jnp.dot(middle, out_weight[update], preferred_element_type=jnp.float32)  15.7 us
    reduce_sum x4, other arithmetic, layer_norm(): variance = jnp.mean(centred * centred, -1, keepdims=True)  13.4 us
    unnamed x22, local copies, waits for them, and re-layouts  11 us
    another operation x2, local copies, waits for them, and re-layouts, finish(): mixed = jnp.transpose(mixed_major, (1, 2, 0))  10.8 us
    reduce_sum x3, other arithmetic, layer_norm(): mean = jnp.mean(values, -1, keepdims=True)  10.3 us
    another operation x2, other arithmetic, channel_body(): jnp.transpose(right, (0, 2, 1))  8.65 us
    another operation x2, local copies, waits for them, and re-layouts, channel_body(): jnp.transpose(left, (0, 2, 1))  8.27 us

profile of v1, /device:TPU:25, one launch (start us, length us, event | category | flops | bytes accessed | tf_op | source)
XLA Modules:
  0.0 402.0 jit_solution(7887627021899168514)
XLA Ops:
  0.0 0.8 slice_bitcast_fusion.2
  0.8 0.8 slice_bitcast_fusion.3
  1.5 0.8 slice_bitcast_fusion
  2.3 0.8 slice_reduce_fusion
  3.1 3.3 reduce_sum.72
  6.4 0.1 copy.63
  6.5 0.1 copy.64
  6.6 4.0 multiply_reduce_fusion.3
  10.6 0.0 copy-start.9
  10.6 0.1 copy.65
  10.7 0.1 copy.66
  10.8 5.8 %add_convert_fusion.3 = bf16[128,64,128]{2,1,0:T(8,128)(2,1)S(1)} fusion(f32[128,64,128]{2,1,0:T(8,128)} %param.9, f32[128]{0:T(128)S(1)} %get-tuple-element.20, f32[128]{0:T(128)S(1)} %get-tuple-element.23, f32[128,64]{1,0:T(8,128)S(1)} %copy.66, f32[128,64]{1,0:T(8,128)S(1)} %copy.64), kind=kLoop, calls=%fused_computation.48 | loop fusion | flops 5242880 | bytes 6358016 | tf_op jit(solution)/shard_map/convert_element_type | solution.py:185
  16.6 0.0 copy-done.9
  16.6 4.0 broadcast_add_fusion.1
  20.6 0.0 copy-start.3
  20.6 4.4 %fusion.40 = (bf16[128,64,128]{0,2,1:T(8,128)(2,1)}, bf16[128,64,128]{0,2,1:T(8,128)(2,1)}) fusion(f32[128,64,640]{2,0,1:T(8,128)S(1)} %broadcast_add_fusion.1), kind=kLoop, calls=%fused_computation.66 | loop fusion | flops 10485760 | bytes 20971520 | tf_op jit(solution)/shard_map/transpose;transpose | solution.py:244
  25.0 3.8 copy-done.3
  28.8 3.3 copy.69
  32.1 4.1 %copy.68 = bf16[128,64,128]{2,1,0:T(8,128)(2,1)} copy(bf16[128,64,128]{0,2,1:T(8,128)(2,1)} %get-tuple-element.10) | data formatting | bytes 4194304 | tf_op jit(solution)/shard_map/transpose;transpose | solution.py:244
  36.2 0.0 copy-start
  36.2 1.6 copy-done
  37.8 145.7 %triangle_0.1 = bf16[32,4,64,128]{3,2,1,0:T(8,128)(2,1)S(1)} custom-call(bf16[32,4,64,128]{3,2,1,0:T(8,128)(2,1)S(1)} %bitcast.77, bf16[32,4,64,128]{3,2,1,0:T(8,128)(2,1)S(1)} %bitcast.75), custom_call_target="tpu_custom_call" | custom-call | tf_op jit(solution)/shard_map/triangle_0/pallas_call | solution.py:153
  183.5 2.6 bitcast_convert_fusion.1
  186.1 5.4 %copy.70 = f32[128,64,128]{0,2,1:T(8,128)} copy(f32[128,64,128]{2,1,0:T(8,128)} %bitcast_convert_fusion.1) | data formatting | bytes 8388608 | tf_op jit(solution)/shard_map/transpose;transpose | solution.py:202
  191.5 0.0 copy-start.4
  191.5 0.0 copy-start.5
  191.5 0.0 copy-start.10
  191.5 3.5 bitcast_reduce_fusion.1
  195.1 4.2 %multiply_reduce_fusion.2 = f32[128,64]{0,1:T(8,128)S(1)} fusion(f32[128,64,128]{0,2,1:T(8,128)} %copy.70, f32[128,64]{0,1:T(8,128)S(1)} %broadcast_multiply_fusion.2), kind=kLoop, calls=%fused_computation.47 | loop fusion | flops 3137536 | bytes 4259840 | tf_op jit(solution)/shard_map/reduce_sum | solution.py:179
  199.2 0.0 copy-done.4
  199.2 0.0 copy-done.5
  199.3 0.0 copy-done.10
  199.3 8.7 %fusion.51 = (f32[128,64]{0,1:T(8,128)S(1)}, f32[128,64,128]{2,0,1:T(8,128)S(1)}) fusion(f32[128]{0:T(128)S(1)} %get-tuple-element.16, bf16[2,128,128]{2,1,0:T(8,128)(2,1)S(1)} %copy-done.10, f32[128,64,128]{0,2,1:T(8,128)S(1)} %copy-done.5, f32[128]{0:T(128)S(1)} %get-tuple-element.25, f32[128]{0:T(128)S(1)} %get-tuple-element.12, ...), kind=kOutput, calls=%fused_computation.97 | convolution fusion | flops 281010176 | bytes 16909824 | tf_op jit(solution)/shard_map/dot_general | solution.py:205
  207.9 0.0 copy-start.7
  208.0 2.6 multiply_reduce_fusion.1
  210.6 3.5 broadcast_add_fusion
  214.1 0.0 copy-done.7
  214.1 0.0 copy-start.2
  214.1 4.3 %fusion.42 = (bf16[128,64,128]{0,2,1:T(8,128)(2,1)}, bf16[128,64,128]{0,2,1:T(8,128)(2,1)}) fusion(f32[128,64,640]{2,0,1:T(8,128)S(1)} %broadcast_add_fusion), kind=kLoop, calls=%fused_computation.68 | loop fusion | flops 10485760 | bytes 20971520 | tf_op jit(solution)/shard_map/transpose;transpose | solution.py:244
  218.4 4.0 copy-done.2
  222.3 3.3 copy.75
  225.6 4.2 %copy.74 = bf16[128,64,128]{2,1,0:T(8,128)(2,1)} copy(bf16[128,64,128]{0,2,1:T(8,128)(2,1)} %get-tuple-element.8) | data formatting | bytes 4194304 | tf_op jit(solution)/shard_map/transpose;transpose | solution.py:244
  229.8 0.0 copy-start.1
  229.8 1.6 copy-done.1
  231.4 145.0 %triangle_1.1 = bf16[32,4,64,128]{3,2,1,0:T(8,128)(2,1)S(1)} custom-call(bf16[32,4,64,128]{3,2,1,0:T(8,128)(2,1)S(1)} %bitcast.78, bf16[32,4,64,128]{3,2,1,0:T(8,128)(2,1)S(1)} %bitcast.76), custom_call_target="tpu_custom_call" | custom-call | tf_op jit(solution)/shard_map/triangle_1/pallas_call | solution.py:153
  376.4 2.6 bitcast_convert_fusion
  379.0 5.4 %copy.76 = f32[128,64,128]{0,2,1:T(8,128)} copy(f32[128,64,128]{2,1,0:T(8,128)} %bitcast_convert_fusion) | data formatting | bytes 8388608 | tf_op jit(solution)/shard_map/transpose;transpose | solution.py:202
  384.4 0.0 copy-start.6
  384.4 0.0 copy-start.8
  384.4 3.5 bitcast_reduce_fusion
  387.9 0.0 copy-done.6
  387.9 2.6 multiply_reduce_fusion
  390.6 0.0 copy-done.8
  390.6 7.0 %fusion.12 = f32[128,64,128]{2,0,1:T(8,128)S(1)} fusion(f32[128,64,128]{2,0,1:T(8,128)S(1)} %copy-done.8, f32[128,64,640]{2,0,1:T(8,128)} %copy-done.2, f32[128,64,128]{0,2,1:T(8,128)S(1)} %copy-done.6, f32[128]{0:T(128)S(1)} %get-tuple-element.15, f32[128]{0:T(128)S(1)} %get-tuple-element.26, f32[128]{0:T(128)S(1)} %get-tuple-element.11, ...), kind=kOutput, calls=%fused_computation.19 | convolution fusion | flops 279969792 | bytes 16877056 | tf_op jit(solution)/shard_map/dot_general | solution.py:205
  397.6 4.4 %copy.77 = f32[128,64,128]{2,1,0:T(8,128)} copy(f32[128,64,128]{2,0,1:T(8,128)S(1)} %fusion.12) | data formatting | bytes 8388608 | tf_op jit(solution)/shard_map/add | solution.py:207
  (8 shorter events, 0.1 us)
Async XLA Ops:
  10.6 6.0 %copy-start.9 = (bf16[2,128,640]{2,1,0:T(8,128)(2,1)S(1)}, bf16[2,128,640]{2,1,0:T(8,128)(2,1)}, u32[]{:S(2)}) copy-start(bf16[2,128,640]{2,1,0:T(8,128)(2,1)} %param.12) | copy-start | bytes 983044
  20.6 8.2 %copy-start.3 = (f32[128,64,640]{2,0,1:T(8,128)}, f32[128,64,640]{2,0,1:T(8,128)S(1)}, u32[]{:S(2)}) copy-start(f32[128,64,640]{2,0,1:T(8,128)S(1)} %broadcast_add_fusion.1) | copy-start | bytes 62914564
  36.2 1.6 copy-start
  191.5 7.7 %copy-start.4 = (f32[128,64,128]{2,1,0:T(8,128)S(1)}, f32[128,64,128]{2,1,0:T(8,128)}, u32[]{:S(2)}) copy-start(f32[128,64,128]{2,1,0:T(8,128)} %param.9) | copy-start | bytes 12582916
  191.5 7.7 %copy-start.5 = (f32[128,64,128]{0,2,1:T(8,128)S(1)}, f32[128,64,128]{0,2,1:T(8,128)}, u32[]{:S(2)}) copy-start(f32[128,64,128]{0,2,1:T(8,128)} %copy.70) | copy-start | bytes 12582916
  191.5 7.7 %copy-start.10 = (bf16[2,128,128]{2,1,0:T(8,128)(2,1)S(1)}, bf16[2,128,128]{2,1,0:T(8,128)(2,1)}, u32[]{:S(2)}) copy-start(bf16[2,128,128]{2,1,0:T(8,128)(2,1)} %param.16) | copy-start | bytes 196612
  207.9 6.2 %copy-start.7 = (f32[128,64,128]{2,0,1:T(8,128)}, f32[128,64,128]{2,0,1:T(8,128)S(1)}, u32[]{:S(2)}) copy-start(f32[128,64,128]{2,0,1:T(8,128)S(1)} %get-tuple-element.22) | copy-start | bytes 12582916
  214.1 8.2 %copy-start.2 = (f32[128,64,640]{2,0,1:T(8,128)}, f32[128,64,640]{2,0,1:T(8,128)S(1)}, u32[]{:S(2)}) copy-start(f32[128,64,640]{2,0,1:T(8,128)S(1)} %broadcast_add_fusion) | copy-start | bytes 62914564
  229.8 1.6 copy-start.1
  384.4 3.5 copy-start.6
  384.4 6.2 %copy-start.8 = (f32[128,64,128]{2,0,1:T(8,128)S(1)}, f32[128,64,128]{2,0,1:T(8,128)}, u32[]{:S(2)}) copy-start(f32[128,64,128]{2,0,1:T(8,128)} %copy-done.7) | copy-start | bytes 12582916

commit v2 on v1

--- a/solution.py
+++ b/solution.py
@@ -233,19 +233,166 @@
     return finish(state, mixed, gate, 1, mid_gain, mid_bias, out_weight, out_bias)
 
 
+CHUNK = 16
+
+
+def take(ref, b):
+    n, chunk, m = ref.shape
+    return ref.reshape(n * chunk, m)[pl.ds(b, n, stride=chunk), :]
+
+
+def put(ref, b, value):
+    n, chunk, m = ref.shape
+    ref.reshape(n * chunk, m)[pl.ds(b, n, stride=chunk), :] = value
+
+
+def project_plane(plane, gain, offset, weights_t, bias_t, gate_weight, gate_bias):
+    normed = layer_norm(plane, gain, offset).astype(jnp.bfloat16)
+    proj_t = (
+        lax.dot_general(
+            weights_t, normed, (((1,), (1,)), ((), ())), preferred_element_type=jnp.float32
+        )
+        + bias_t
+    )
+    hidden = proj_t.shape[0] // 4
+    parts = [proj_t[n * hidden : (n + 1) * hidden] for n in range(4)]
+    gate = jax.nn.sigmoid(
+        jnp.dot(normed, gate_weight, preferred_element_type=jnp.float32) + gate_bias
+    )
+    return jax.nn.sigmoid(parts[1]) * parts[0], jax.nn.sigmoid(parts[3]) * parts[2], gate
+
+
+def finish_plane(plane, mixed, gate, gain_t, offset_t, weight, bias):
+    mean = jnp.mean(mixed, 0, keepdims=True)
+    centred = mixed - mean
+    variance = jnp.mean(centred * centred, 0, keepdims=True)
+    middle = (centred * lax.rsqrt(variance + 1e-05) * gain_t + offset_t).astype(jnp.bfloat16)
+    outcome = (
+        lax.dot_general(
+            middle, weight, (((0,), (0,)), ((), ())), preferred_element_type=jnp.float32
+        )
+        + bias
+    )
+    return plane + gate * outcome
+
+
+def first_kernel(pair_ref, *refs):
+    before, (left_ref, right_ref, gate_ref, left_held, right_held) = refs[:6], refs[6:]
+
+    def step(b, carry):
+        left, right, gate = project_plane(take(pair_ref, b), *[ref[...] for ref in before])
+        put(left_held, b, left)
+        put(right_held, b, right)
+        gate_ref[b] = gate
+        return carry
+
+    lax.fori_loop(0, CHUNK, step, 0, unroll=2)
+    left_ref[...] = left_held[...].astype(jnp.bfloat16)
+    right_ref[...] = right_held[...].astype(jnp.bfloat16)
+
+
+def middle_kernel(pair_ref, mixed_ref, old_gate_ref, *refs):
+    after, before = refs[:4], refs[4:10]
+    state_ref, left_ref, right_ref, gate_ref, left_held, right_held, mixed_held = refs[10:]
+    mixed_held[...] = mixed_ref[...].astype(jnp.float32)
+
+    def step(b, carry):
+        state = finish_plane(
+            take(pair_ref, b), take(mixed_held, b), old_gate_ref[b], *[ref[...] for ref in after]
+        )
+        state_ref[b] = state
+        left, right, gate = project_plane(state, *[ref[...] for ref in before])
+        put(left_held, b, left)
+        put(right_held, b, right)
+        gate_ref[b] = gate
+        return carry
+
+    lax.fori_loop(0, CHUNK, step, 0, unroll=2)
+    left_ref[...] = left_held[...].astype(jnp.bfloat16)
+    right_ref[...] = right_held[...].astype(jnp.bfloat16)
+
+
+def last_kernel(state_ref, mixed_ref, gate_ref, *refs):
+    after, (out_ref, mixed_held) = refs[:4], refs[4:]
+    mixed_held[...] = mixed_ref[...].astype(jnp.float32)
+
+    def step(b, carry):
+        put(
+            out_ref,
+            b,
+            finish_plane(
+                state_ref[b], take(mixed_held, b), gate_ref[b], *[ref[...] for ref in after]
+            ),
+        )
+        return carry
+
+    lax.fori_loop(0, CHUNK, step, 0, unroll=2)
+
+
+def pointwise(kernel, name, depth, streams, constants, outs, held):
+    def spec(shape, where):
+        block = tuple(CHUNK if n == where else extent for n, extent in enumerate(shape))
+        return pl.BlockSpec(block, lambda i: tuple(i if n == where else 0 for n in range(3)))
+
+    def fixed(array):
+        return pl.BlockSpec(array.shape, lambda i: (0,) * array.ndim)
+
+    return pl.pallas_call(
+        kernel,
+        grid=(depth // CHUNK,),
+        out_shape=[shape for shape, _ in outs],
+        in_specs=[spec(array.shape, where) for array, where in streams]
+        + [fixed(array) for array in constants],
+        out_specs=[spec(shape.shape, where) for shape, where in outs],
+        scratch_shapes=[pltpu.VMEM(shape, jnp.float32) for shape in held],
+        compiler_params=pltpu.CompilerParams(vmem_limit_bytes=48 * 1024 * 1024),
+        name=name,
+    )(*[array for array, _ in streams], *constants)
+
+
 def channel_body(
     rows, cols, pair, in_gain, in_bias, proj_weight, proj_bias, mid_gain, mid_bias, out_weight,
     out_bias,
 ):
-    state = pair
-    for update in range(2):
-        left, right, gate = projections(state, update, in_gain, in_bias, proj_weight, proj_bias)
-        mixed = triangle(
-            update, rows, cols, jnp.transpose(left, (0, 2, 1)), jnp.transpose(right, (0, 2, 1))
-        )
-        mixed = jnp.transpose(mixed.astype(jnp.float32), (0, 2, 1))
-        state = finish(state, mixed, gate, update, mid_gain, mid_bias, out_weight, out_bias)
-    return state
+    width, depth, wide = pair.shape
+    hidden = out_weight.shape[1]
+
+    def before(update):
+        weight, bias = proj_weight[update], proj_bias[update]
+        return [
+            in_gain[update][None],
+            in_bias[update][None],
+            weight[:, : 4 * hidden].T,
+            jnp.broadcast_to(bias[: 4 * hidden, None], (4 * hidden, width)),
+            weight[:, 4 * hidden :],
+            bias[None, 4 * hidden :],
+        ]
+
+    def after(update):
+        return [
+            jnp.broadcast_to(mid_gain[update][:, None], (hidden, width)),
+            jnp.broadcast_to(mid_bias[update][:, None], (hidden, width)),
+            out_weight[update],
+            out_bias[update][None],
+        ]
+
+    major = (jax.ShapeDtypeStruct((hidden, depth, width), jnp.bfloat16), 1)
+    planes = (jax.ShapeDtypeStruct((depth, width, wide), jnp.float32), 0)
+    held = (hidden, CHUNK, width)
+    left, right, gate = pointwise(
+        first_kernel, "first", depth, [(pair, 1)], before(0), [major, major, planes], [held] * 2
+    )
+    mixed = triangle(0, rows, cols, left, right)
+    state, left, right, gate = pointwise(
+        middle_kernel, "middle", depth, [(pair, 1), (mixed, 1), (gate, 0)],
+        after(0) + before(1), [planes, major, major, planes], [held] * 3,
+    )
+    mixed = triangle(1, rows, cols, left, right)
+    (updated,) = pointwise(
+        last_kernel, "last", depth, [(state, 0), (mixed, 1), (gate, 0)], after(1),
+        [(jax.ShapeDtypeStruct(pair.shape, jnp.float32), 1)], [held],
+    )
+    return updated
 
 
 def solution(mesh):
@@ -255,7 +402,8 @@
     def run(*arrays):
         hidden = arrays[7].shape[1]
         local = functools.partial(channel_body, rows, cols)
-        if hidden % (rows * cols) != 0:
+        depth = arrays[0].shape[1] // cols
+        if hidden % (rows * cols) != 0 or depth % CHUNK != 0:
             local = body
         return jax.shard_map(
             local, mesh=mesh, in_specs=placed, out_specs=P("row", "col", None), check_vma=False

time: 403 us -> 368 us (0.913)
  Pallas kernels: 291 us -> 362 us
  other arithmetic: 43.4 us -> 0 us
  local copies, waits for them, and re-layouts: 44.5 us -> 5.5 us
  matrix products: 23.1 us -> 0 us
    pallas_call x0 -> x3, Pallas kernels: none -> 70.9 us  [pointwise(): pl.pallas_call(kernel, grid=(depth // CHUNK,), out_shape=[shape for shape...]
    another operation x6 -> x0, local copies, waits for them, and re-layouts: 25.7 us -> none  [the longest x2 10.8 us: finish(): mixed = jnp.transpose(mixed_major, (1, 2, 0))]
    reduce_sum x7 -> x0, other arithmetic: 23.7 us -> none  [the longest x4 13.4 us: layer_norm(): variance = jnp.mean(centred * centred, -1, keepdims=True)]
    dot_general x4 -> x0, matrix products: 23.1 us -> none  [the longest x2 15.7 us: finish(): jnp.dot(middle, out_weight[update], preferred_element_type=jnp.float32)]
    another operation x4 -> x0, other arithmetic: 13.8 us -> none  [the longest x2 8.65 us: channel_body(): jnp.transpose(right, (0, 2, 1))]
    unnamed x22 -> x8, local copies, waits for them, and re-layouts: 11 us -> 1.37 us
    add x3 -> x0, local copies, waits for them, and re-layouts: 5.97 us -> none  [the longest x1 4.44 us: finish(): return state + gate * outcome]
    convert_element_type x1 -> x0, other arithmetic: 5.78 us -> none  [projections(): layer_norm(state, in_gain[update], in_bias[update]).astype(jnp.bfloat16)]
where the time goes in v2:
time: 368 us
  Pallas kernels  362 us (98%)
  local copies, waits for them, and re-layouts  5.5 us (1%)
    pallas_call x2, Pallas kernels, triangle(): pl.pallas_call(functools.partial(triangle_kernel, update, rows, cols), ou...  291 us
    pallas_call x3, Pallas kernels, pointwise(): pl.pallas_call(kernel, grid=(depth // CHUNK,), out_shape=[shape for shape...  70.9 us

profile of v2, /device:TPU:25, one launch (start us, length us, event | category | flops | bytes accessed | tf_op | source)
XLA Modules:
  0.0 367.8 jit_solution(17789545436490222997)
XLA Ops:
  0.0 1.0 slice_bitcast_fusion
  1.1 0.1 copy.10.refs_2_
  1.2 0.8 fusion
  1.9 0.8 fusion.2
  2.7 0.8 fusion.1
  3.5 0.1 broadcast_in_dim.47.refs_3_
  3.6 20.1 %first.1 = (bf16[128,64,128]{2,1,0:T(8,128)(2,1)S(1)}, bf16[128,64,128]{2,1,0:T(8,128)(2,1)S(1)}, f32[64,128,128]{2,1,0:T(8,128)}) custom-call(f32[128,64,128]{2,1,0:T(8,128)} %pair_ref.3, f32[1,128]{1,0:T(1,128)S(1)} %get-tuple-element.41.refs_0_, f32[1,128]{1,0:T(1,128)S(1)} %get-tuple-element.39.refs_1_, bf16[512,128]{1,0:T(8,128)(2,1)S(1)} %copy.10.refs_2_, ...), custom_call_target="tpu_custom_call" | custom-call | tf_op jit(solution)/shard_map/first/pallas_call | solution.py:340
  23.7 0.0 copy-start.2
  23.7 0.0 copy-start.3
  23.7 0.0 copy-start.1
  23.7 146.0 %triangle_0.1 = bf16[32,4,64,128]{3,2,1,0:T(8,128)(2,1)S(1)} custom-call(bf16[32,4,64,128]{3,2,1,0:T(8,128)(2,1)S(1)} %bitcast.32, bf16[32,4,64,128]{3,2,1,0:T(8,128)(2,1)S(1)} %bitcast.33), custom_call_target="tpu_custom_call" | custom-call | tf_op jit(solution)/shard_map/triangle_0/pallas_call | solution.py:153
  169.7 0.0 copy-start
  169.7 1.4 copy-done
  171.0 0.1 copy.11.refs_6_
  171.2 0.1 broadcast_in_dim.53.refs_7_
  171.3 0.0 copy-done.2
  171.3 0.1 broadcast_in_dim.49.refs_0_
  171.4 0.0 copy-done.3
  171.4 0.1 broadcast_in_dim.51.refs_1_
  171.5 0.0 copy-done.1
  171.5 37.4 %middle.1 = (f32[64,128,128]{2,1,0:T(8,128)}, bf16[128,64,128]{2,1,0:T(8,128)(2,1)S(1)}, bf16[128,64,128]{2,1,0:T(8,128)(2,1)S(1)}, f32[64,128,128]{2,1,0:T(8,128)}) custom-call(f32[128,64,128]{2,1,0:T(8,128)} %pair_ref.3, bf16[128,64,128]{2,1,0:T(8,128)(2,1)} %bitcast.28, f32[64,128,128]{2,1,0:T(8,128)} %get-tuple-element.14.old_gate_ref, ...), custom_call_target="tpu_custom_call" | custom-call | tf_op jit(solution)/shard_map/middle/pallas_call | solution.py:340
  208.9 145.3 %triangle_1.1 = bf16[32,4,64,128]{3,2,1,0:T(8,128)(2,1)S(1)} custom-call(bf16[32,4,64,128]{3,2,1,0:T(8,128)(2,1)S(1)} %bitcast.30, bf16[32,4,64,128]{3,2,1,0:T(8,128)(2,1)S(1)} %bitcast.31), custom_call_target="tpu_custom_call" | custom-call | tf_op jit(solution)/shard_map/triangle_1/pallas_call | solution.py:153
  354.2 0.1 broadcast_in_dim.55.refs_0_
  354.2 0.1 broadcast_in_dim.57.refs_1_
  354.3 13.5 %last.1 = f32[128,64,128]{2,1,0:T(8,128)} custom-call(f32[64,128,128]{2,1,0:T(8,128)} %get-tuple-element.15.state_ref, bf16[128,64,128]{2,1,0:T(8,128)(2,1)S(1)} %bitcast.29, f32[64,128,128]{2,1,0:T(8,128)} %get-tuple-element.18.gate_ref, f32[128,128]{1,0:T(8,128)S(1)} %broadcast_in_dim.55.refs_0_, f32[128,128]{1,0:T(8,128)S(1)} %broadcast_in_dim.57.refs_1_, ...), custom_call_target="tpu_custom_call" | custom-call | tf_op jit(solution)/shard_map/last/pallas_call | solution.py:340
  (6 shorter events, 0.0 us)
Async XLA Ops:
  23.7 147.6 %copy-start.2 = (f32[2,128]{1,0:T(2,128)S(1)}, f32[2,128]{1,0:T(2,128)}, u32[]{:S(2)}) copy-start(f32[2,128]{1,0:T(2,128)} %param.14) | copy-start | bytes 3076
  23.7 147.7 %copy-start.3 = (f32[2,128]{1,0:T(2,128)S(1)}, f32[2,128]{1,0:T(2,128)}, u32[]{:S(2)}) copy-start(f32[2,128]{1,0:T(2,128)} %param.15) | copy-start | bytes 3076
  23.7 147.8 %copy-start.1 = (bf16[2,128,128]{2,1,0:T(8,128)(2,1)S(1)}, bf16[2,128,128]{2,1,0:T(8,128)(2,1)}, u32[]{:S(2)}) copy-start(bf16[2,128,128]{2,1,0:T(8,128)(2,1)} %param.16) | copy-start | bytes 196612
  169.7 1.4 copy-start

commit v3 on v2

--- a/solution.py
+++ b/solution.py
@@ -234,6 +234,11 @@
 
 
 CHUNK = 16
+UNROLL = 16
+
+
+def sigmoid(x):
+    return 0.5 * jnp.tanh(0.5 * x) + 0.5
 
 
 def take(ref, b):
@@ -256,10 +261,10 @@
     )
     hidden = proj_t.shape[0] // 4
     parts = [proj_t[n * hidden : (n + 1) * hidden] for n in range(4)]
-    gate = jax.nn.sigmoid(
+    gate = sigmoid(
         jnp.dot(normed, gate_weight, preferred_element_type=jnp.float32) + gate_bias
     )
-    return jax.nn.sigmoid(parts[1]) * parts[0], jax.nn.sigmoid(parts[3]) * parts[2], gate
+    return sigmoid(parts[1]) * parts[0], sigmoid(parts[3]) * parts[2], gate
 
 
 def finish_plane(plane, mixed, gate, gain_t, offset_t, weight, bias):
@@ -286,7 +291,7 @@
         gate_ref[b] = gate
         return carry
 
-    lax.fori_loop(0, CHUNK, step, 0, unroll=2)
+    lax.fori_loop(0, CHUNK, step, 0, unroll=UNROLL)
     left_ref[...] = left_held[...].astype(jnp.bfloat16)
     right_ref[...] = right_held[...].astype(jnp.bfloat16)
 
@@ -307,7 +312,7 @@
         gate_ref[b] = gate
         return carry
 
-    lax.fori_loop(0, CHUNK, step, 0, unroll=2)
+    lax.fori_loop(0, CHUNK, step, 0, unroll=UNROLL)
     left_ref[...] = left_held[...].astype(jnp.bfloat16)
     right_ref[...] = right_held[...].astype(jnp.bfloat16)
 
@@ -326,7 +331,7 @@
         )
         return carry
 
-    lax.fori_loop(0, CHUNK, step, 0, unroll=2)
+    lax.fori_loop(0, CHUNK, step, 0, unroll=UNROLL)
 
 
 def pointwise(kernel, name, depth, streams, constants, outs, held):

time: 368 us -> 346 us (0.940)
  Pallas kernels: 362 us -> 340 us
    pallas_call x3, Pallas kernels: 70.9 us -> 49.1 us  [pointwise(): pl.pallas_call(kernel, grid=(depth // CHUNK,), out_shape=[shape for shape...]
where the time goes in v3:
time: 346 us
  Pallas kernels  340 us (98%)
  local copies, waits for them, and re-layouts  5.5 us (2%)
    pallas_call x2, Pallas kernels, triangle(): pl.pallas_call(functools.partial(triangle_kernel, update, rows, cols), ou...  291 us
    pallas_call x3, Pallas kernels, pointwise(): pl.pallas_call(kernel, grid=(depth // CHUNK,), out_shape=[shape for shape...  49.1 us

profile of v3, /device:TPU:25, one launch (start us, length us, event | category | flops | bytes accessed | tf_op | source)
XLA Modules:
  0.0 346.0 jit_solution(5697268726185880643)
XLA Ops:
  0.0 1.0 slice_bitcast_fusion
  1.1 0.1 copy.10.refs_2_
  1.2 0.8 fusion
  1.9 0.8 fusion.2
  2.7 0.8 fusion.1
  3.5 0.1 broadcast_in_dim.47.refs_3_
  3.6 12.7 %first.1 = (bf16[128,64,128]{2,1,0:T(8,128)(2,1)S(1)}, bf16[128,64,128]{2,1,0:T(8,128)(2,1)S(1)}, f32[64,128,128]{2,1,0:T(8,128)}) custom-call(f32[128,64,128]{2,1,0:T(8,128)} %pair_ref.3, f32[1,128]{1,0:T(1,128)S(1)} %get-tuple-element.41.refs_0_, f32[1,128]{1,0:T(1,128)S(1)} %get-tuple-element.39.refs_1_, bf16[512,128]{1,0:T(8,128)(2,1)S(1)} %copy.10.refs_2_, ...), custom_call_target="tpu_custom_call" | custom-call | tf_op jit(solution)/shard_map/first/pallas_call | solution.py:345
  16.3 0.0 copy-start.2
  16.3 0.0 copy-start.3
  16.3 0.0 copy-start.1
  16.3 146.0 %triangle_0.1 = bf16[32,4,64,128]{3,2,1,0:T(8,128)(2,1)S(1)} custom-call(bf16[32,4,64,128]{3,2,1,0:T(8,128)(2,1)S(1)} %bitcast.32, bf16[32,4,64,128]{3,2,1,0:T(8,128)(2,1)S(1)} %bitcast.33), custom_call_target="tpu_custom_call" | custom-call | tf_op jit(solution)/shard_map/triangle_0/pallas_call | solution.py:153
  162.3 0.0 copy-start
  162.3 1.4 copy-done
  163.7 0.1 copy.11.refs_6_
  163.8 0.1 broadcast_in_dim.53.refs_7_
  163.9 0.0 copy-done.2
  164.0 0.1 broadcast_in_dim.49.refs_0_
  164.0 0.0 copy-done.3
  164.1 0.1 broadcast_in_dim.51.refs_1_
  164.1 0.0 copy-done.1
  164.2 28.3 %middle.1 = (f32[64,128,128]{2,1,0:T(8,128)}, bf16[128,64,128]{2,1,0:T(8,128)(2,1)S(1)}, bf16[128,64,128]{2,1,0:T(8,128)(2,1)S(1)}, f32[64,128,128]{2,1,0:T(8,128)}) custom-call(f32[128,64,128]{2,1,0:T(8,128)} %pair_ref.3, bf16[128,64,128]{2,1,0:T(8,128)(2,1)} %bitcast.28, f32[64,128,128]{2,1,0:T(8,128)} %get-tuple-element.14.old_gate_ref, ...), custom_call_target="tpu_custom_call" | custom-call | tf_op jit(solution)/shard_map/middle/pallas_call | solution.py:345
  192.4 145.3 %triangle_1.1 = bf16[32,4,64,128]{3,2,1,0:T(8,128)(2,1)S(1)} custom-call(bf16[32,4,64,128]{3,2,1,0:T(8,128)(2,1)S(1)} %bitcast.30, bf16[32,4,64,128]{3,2,1,0:T(8,128)(2,1)S(1)} %bitcast.31), custom_call_target="tpu_custom_call" | custom-call | tf_op jit(solution)/shard_map/triangle_1/pallas_call | solution.py:153
  337.7 0.1 broadcast_in_dim.55.refs_0_
  337.8 0.1 broadcast_in_dim.57.refs_1_
  337.8 8.2 %last.1 = f32[128,64,128]{2,1,0:T(8,128)} custom-call(f32[64,128,128]{2,1,0:T(8,128)} %get-tuple-element.15.state_ref, bf16[128,64,128]{2,1,0:T(8,128)(2,1)S(1)} %bitcast.29, f32[64,128,128]{2,1,0:T(8,128)} %get-tuple-element.18.gate_ref, f32[128,128]{1,0:T(8,128)S(1)} %broadcast_in_dim.55.refs_0_, f32[128,128]{1,0:T(8,128)S(1)} %broadcast_in_dim.57.refs_1_, ...), custom_call_target="tpu_custom_call" | custom-call | tf_op jit(solution)/shard_map/last/pallas_call | solution.py:345
  (6 shorter events, 0.0 us)
Async XLA Ops:
  16.3 147.6 %copy-start.2 = (f32[2,128]{1,0:T(2,128)S(1)}, f32[2,128]{1,0:T(2,128)}, u32[]{:S(2)}) copy-start(f32[2,128]{1,0:T(2,128)} %param.14) | copy-start | bytes 3076
  16.3 147.7 %copy-start.3 = (f32[2,128]{1,0:T(2,128)S(1)}, f32[2,128]{1,0:T(2,128)}, u32[]{:S(2)}) copy-start(f32[2,128]{1,0:T(2,128)} %param.15) | copy-start | bytes 3076
  16.3 147.8 %copy-start.1 = (bf16[2,128,128]{2,1,0:T(8,128)(2,1)S(1)}, bf16[2,128,128]{2,1,0:T(8,128)(2,1)}, u32[]{:S(2)}) copy-start(bf16[2,128,128]{2,1,0:T(8,128)(2,1)} %param.16) | copy-start | bytes 196612
  162.3 1.4 copy-start
